TPU v7x, 32 devices: a whole 2x2x4 slice. The times are simulated.
32 devices in a mesh: ctx: 4 (over y, x), head: 8 (over z, core).
Axes of the slice: x: 2, y: 2, z: 4, core: 2. Of those that a mesh axis runs over, the one named last changes fastest.
Arguments:
- state: bfloat16 [4096, 2048], P('ctx'), may hold values from -6 to 6
- norm_gain: bfloat16 [2048], replicated, may hold values from 0.5 to 1.5
- w_qkv: bfloat16 [3, 2048, 2048], P(None, None, 'head'), may hold values from -2 to 2
- w_out: bfloat16 [2048, 2048], P('head'), may hold values from -0.125 to 0.125
- probe: bfloat16 [4096, 2048], P('ctx'), may hold values from -6 to 6
- noise: bfloat16 [4096, 2048], P(('ctx', 'head')), may hold values from -6 to 6
- segment_ids: int32 [4096], P('ctx'), may hold values from 0 to 2, never falling along the last dimension, each value on 1 to 3072 neighbouring positions
Outputs:
- new_state: float32 [4096, 2048], P(('ctx', 'head'))
Inputs may be any that keep to these rules, and one draw needn't show every extreme that they name: `segment_ids`: segment numbers never fall along the sequence; a segment holds at most 3072 positions.
All inputs are finite; a program needn't handle non-finite values.
Results may differ from a plain program's by a relative error of at most 0.011.
Values may be sent and summed in bfloat16 or wider, within the bound.
A program may use at most 128 MiB of HBM per device.

v0:
```python
import jax
import jax.numpy as jnp
from jax import lax
from jax.sharding import PartitionSpec as P

HEAD_DIM = 128
EPSILON = 1e-05
STEP_SIZE = 0.25
NEGATIVE = -1e30


def row_scale(matrix):
    return lax.rsqrt(jnp.mean(matrix * matrix, axis=-1, keepdims=True) + EPSILON)


def readout_grad(layer_out, probe_full):
    scale_y = row_scale(layer_out)
    return scale_y * probe_full - layer_out * scale_y**3 * jnp.mean(
        probe_full * layer_out, axis=-1, keepdims=True
    )


def over_blocks(block_fn, state_carry, arrays, begin_row, block_limit):
    row_count = arrays[0].shape[0]
    block_size = min(row_count, block_limit)
    number = row_count // block_size
    stacked = tuple((member.reshape((number, block_size) + member.shape[1:]) for member in arrays))
    offsets = begin_row + block_size * jnp.arange(number, dtype=jnp.int32)

    def advance(running, scan_item):
        return (block_fn(running, scan_item[0], scan_item[1]), None)

    state_carry, _ = lax.scan(advance, state_carry, (stacked, offsets))
    return state_carry


def body(state, norm_gain, w_qkv, w_out, probe, noise, segment_ids):
    local_rows, model_width = state.shape
    local_heads = w_qkv.shape[2] // HEAD_DIM
    score_scale = HEAD_DIM ** (-0.5)
    head_count = lax.axis_size("head")
    ctx_index = lax.axis_index("ctx")
    own_rows = local_rows // head_count
    row_start = lax.axis_index("head") * own_rows
    state_f = state.astype(jnp.float32)
    gain_full = norm_gain.astype(jnp.float32)
    inverse = row_scale(state_f)
    normed = (state_f * inverse * gain_full).astype(jnp.bfloat16)
    projected = jnp.einsum("sd,cdn->csn", normed, w_qkv, preferred_element_type=jnp.float32).astype(
        jnp.bfloat16
    )
    query_rows, key_rows, value_rows = (projected[0], projected[1], projected[2])
    queries = query_rows.reshape(local_rows, local_heads, HEAD_DIM).transpose(1, 0, 2)
    query_pos = ctx_index * local_rows + jnp.arange(local_rows, dtype=jnp.int32)

    def visible(key_seg, key_start):
        key_pos = key_start + jnp.arange(key_seg.shape[0], dtype=jnp.int32)
        return (
            (key_pos[None, :] <= query_pos[:, None]) & (key_seg[None, :] == segment_ids[:, None])
        )[None]

    def forward_block(state_carry, key_piece, key_start):
        run_max, run_sum, run_acc = state_carry
        block_rows = key_piece[0].shape[0]
        key_heads = key_piece[0].reshape(block_rows, local_heads, HEAD_DIM)
        value_heads = key_piece[1].reshape(block_rows, local_heads, HEAD_DIM)
        allowed = visible(key_piece[2], key_start)
        scores = (
            jnp.einsum("hqe,khe->hqk", queries, key_heads, preferred_element_type=jnp.float32)
            * score_scale
        )
        scores = jnp.where(allowed, scores, NEGATIVE)
        new_max = jnp.maximum(run_max, jnp.max(scores, axis=-1))
        weights = jnp.where(allowed, jnp.exp(scores - new_max[..., None]), 0.0)
        factor = jnp.exp(run_max - new_max)
        run_sum = run_sum * factor + jnp.sum(weights, axis=-1)
        run_acc = run_acc * factor[..., None] + jnp.einsum(
            "hqk,khe->hqe",
            weights.astype(jnp.bfloat16),
            value_heads,
            preferred_element_type=jnp.float32,
        )
        return (new_max, run_sum, run_acc)

    initial = (
        jnp.full((local_heads, local_rows), NEGATIVE, jnp.float32),
        jnp.zeros((local_heads, local_rows), jnp.float32),
        jnp.zeros((local_heads, local_rows, HEAD_DIM), jnp.float32),
    )
    all_keys, all_values, all_segs = (
        lax.all_gather(key_rows, "ctx", axis=0, tiled=True),
        lax.all_gather(value_rows, "ctx", axis=0, tiled=True),
        lax.all_gather(segment_ids, "ctx", axis=0, tiled=True),
    )
    run_max, run_sum, run_acc = over_blocks(
        forward_block, initial, (all_keys, all_values, all_segs), 0, local_rows
    )
    outputs = (run_acc / run_sum[..., None]).astype(jnp.bfloat16)
    log_totals = run_max + jnp.log(run_sum)
    out_rows = outputs.transpose(1, 0, 2).reshape(local_rows, local_heads * HEAD_DIM)
    state_own = lax.dynamic_slice_in_dim(state_f, row_start, own_rows, 0)
    inverse_own = lax.dynamic_slice_in_dim(inverse, row_start, own_rows, 0)
    term = jnp.dot(out_rows, w_out, preferred_element_type=jnp.float32)
    layer_out = state_f + lax.psum(term.astype(jnp.bfloat16), "head").astype(jnp.float32)
    readout_full = readout_grad(layer_out, probe.astype(jnp.float32))
    readout_half = readout_full.astype(jnp.bfloat16)
    readout_own = lax.dynamic_slice_in_dim(readout_full, row_start, own_rows, 0)
    grads_out = jnp.einsum(
        "sd,hed->hse",
        readout_half,
        w_out.reshape(local_heads, HEAD_DIM, model_width),
        preferred_element_type=jnp.float32,
    ).astype(jnp.bfloat16)
    deltas = jnp.sum(grads_out.astype(jnp.float32) * outputs.astype(jnp.float32), axis=-1)

    def back_block(key_block, value_block, seg_block, key_start):
        block_rows = key_block.shape[0]
        key_heads = key_block.reshape(block_rows, local_heads, HEAD_DIM)
        value_heads = value_block.reshape(block_rows, local_heads, HEAD_DIM)
        allowed = visible(seg_block, key_start)
        scores = (
            jnp.einsum("hqe,khe->hqk", queries, key_heads, preferred_element_type=jnp.float32)
            * score_scale
        )
        probabilities = jnp.where(
            allowed, jnp.exp(jnp.where(allowed, scores, NEGATIVE) - log_totals[..., None]), 0.0
        )
        dprobs = jnp.einsum(
            "hqe,khe->hqk", grads_out, value_heads, preferred_element_type=jnp.float32
        )
        dscores = probabilities * (dprobs - deltas[..., None])
        prob_half = probabilities.astype(jnp.bfloat16)
        dscore_half = dscores.astype(jnp.bfloat16)
        value_part = jnp.einsum(
            "hqk,hqe->khe", prob_half, grads_out, preferred_element_type=jnp.float32
        )
        key_part = (
            jnp.einsum("hqk,hqe->khe", dscore_half, queries, preferred_element_type=jnp.float32)
            * score_scale
        )
        query_part = (
            jnp.einsum("hqk,khe->hqe", dscore_half, key_heads, preferred_element_type=jnp.float32)
            * score_scale
        )
        return (query_part, key_part.reshape(block_rows, -1), value_part.reshape(block_rows, -1))

    query_zero = jnp.zeros((local_heads, local_rows, HEAD_DIM), jnp.float32)

    def add_query(running, key_piece, key_start):
        query_part, _, _ = back_block(key_piece[0], key_piece[1], key_piece[2], key_start)
        return running + query_part

    query_acc = over_blocks(add_query, query_zero, (all_keys, all_values, all_segs), 0, local_rows)
    row_count = local_rows * lax.axis_size("ctx")
    block_size = min(row_count, local_rows)
    number = row_count // block_size

    def one_block(block_index):
        offset = block_index * block_size
        key_block = lax.dynamic_slice_in_dim(all_keys, offset, block_size, 0)
        value_block = lax.dynamic_slice_in_dim(all_values, offset, block_size, 0)
        seg_block = lax.dynamic_slice_in_dim(all_segs, offset, block_size, 0)
        _, key_part, value_part = back_block(key_block, value_block, seg_block, offset)
        return jnp.concatenate([key_part, value_part], axis=1)

    part_rows = lax.map(one_block, jnp.arange(number, dtype=jnp.int32))
    summed = lax.psum_scatter(
        part_rows.reshape(row_count, -1).astype(jnp.bfloat16),
        "ctx",
        scatter_dimension=0,
        tiled=True,
    ).astype(jnp.float32)
    key_sum = summed[:, : local_heads * HEAD_DIM]
    value_sum = summed[:, local_heads * HEAD_DIM :]
    query_grad = (
        query_acc.astype(jnp.bfloat16)
        .transpose(1, 0, 2)
        .reshape(local_rows, local_heads * HEAD_DIM)
    )
    key_grad = key_sum.astype(jnp.bfloat16)
    value_grad = value_sum.astype(jnp.bfloat16)
    running = jnp.einsum("sn,dn->sd", query_grad, w_qkv[0], preferred_element_type=jnp.float32)
    running = running + jnp.einsum(
        "sn,dn->sd", key_grad, w_qkv[1], preferred_element_type=jnp.float32
    )
    normed_grad = lax.psum_scatter(
        (
            running
            + jnp.einsum("sn,dn->sd", value_grad, w_qkv[2], preferred_element_type=jnp.float32)
        ).astype(jnp.bfloat16),
        "head",
        scatter_dimension=0,
        tiled=True,
    ).astype(jnp.float32)
    gain_grad = normed_grad * gain_full
    gradient = (
        readout_own
        + inverse_own * gain_grad
        - state_own * inverse_own**3 * jnp.mean(gain_grad * state_own, axis=-1, keepdims=True)
    )
    return state_own - STEP_SIZE * gradient + jnp.sqrt(2.0 * STEP_SIZE) * noise.astype(jnp.float32)


def solution(mesh):
    placed = (
        P("ctx", None),
        P(),
        P(None, None, "head"),
        P("head", None),
        P("ctx", None),
        P(("ctx", "head"), None),
        P("ctx"),
    )
    return jax.shard_map(
        body, mesh=mesh, in_specs=placed, out_specs=P(("ctx", "head"), None), check_vma=False
    )
```

profile of v0, /device:TPU:0, one launch (start us, length us, event | category | flops | bytes accessed | tf_op | source)
XLA Modules:
  0.0 553.4 jit_solution(13009157587223237203)
XLA Ops:
  10.4 6.9 %fusion.73 = bf16[3,1024,256]{1,2,0:T(8,128)(2,1)S(1)} fusion(bf16[3,2048,256]{2,1,0:T(8,128)(2,1)} %param.15, bf16[1024,2048]{1,0:T(8,128)(2,1)} %param.13, f32[2048]{0:T(1024)S(1)} %convert_element_type.76, f32[1024]{0:T(1024)S(1)} %add_rsqrt_fusion.1), kind=kOutput, calls=%fused_computation.90 | convolution fusion | flops 3230400512 | bytes 8925184 | tf_op jit(solution)/shard_map/sd,cdn->csn/dot_general | solution.py:49
  19.6 10.0 %all_gather.9 = s32[4096]{0:T(1024)S(1)} all-gather(s32[1024]{0:T(1024)S(1)} %copy-done.10), channel_id=1, replica_groups=mesh['ctx'=4,'head'=8] {'ctx'}, dimensions={0}, use_global_device_ids=true | all-gather | bytes 20480 | tf_op jit(solution)/shard_map/all_gather | solution.py:93
  29.6 26.9 %all-gather.5.cloned.1.call-done = bf16[1,4096,256]{1,2,0:T(8,128)(2,1)} async-done(((bf16[1,1024,256]{1,2,0:T(8,128)(2,1)}), bf16[1,4096,256]{1,2,0:T(8,128)(2,1)}) %all-gather.5.cloned.1.call-update) | async-done | bytes 2097168 | tf_op jit(solution)/shard_map/all_gather | solution.py:91
  64.7 28.9 %all-gather.7.cloned.1.call-done = bf16[1,4096,256]{1,2,0:T(8,128)(2,1)} async-done(((bf16[1,1024,256]{1,2,0:T(8,128)(2,1)}), bf16[1,4096,256]{1,2,0:T(8,128)(2,1)}) %all-gather.7.cloned.1.call-update) | async-done | bytes 2097168 | tf_op jit(solution)/shard_map/all_gather | solution.py:92
  101.7 83.2 %while.38 = (s32[]{:T(128)}, f32[2,1024]{1,0:T(2,128)S(1)}, f32[2,1024]{1,0:T(2,128)S(1)}, f32[2,1024,128]{2,1,0:T(8,128)}, s32[4]{0:T(128)S(1)}, /*index=5*/s32...) while((s32[]{:T(128)}, f32[2,1024]{1,0:T(2,128)S(1)}, ...), condition=%wide.region_4.5_spmd.clone, body=%wide.region_1.4_spmd.clone.sunk | while | flops 1104949248 | bytes 70942944 | solution.py:33
  106.4 5.1 fusion.158
  126.4 5.1 fusion.158
  137.4 5.4 fusion.162
  147.5 5.1 fusion.158
  158.5 5.4 fusion.162
  168.6 5.1 fusion.158
  179.5 5.4 fusion.162
  192.7 96.0 %all-reduce.2.cloned.1.call-done = bf16[1024,2048]{1,0:T(8,128)(2,1)} async-done(((bf16[1024,2048]{1,0:T(8,128)(2,1)}), bf16[1024,2048]{1,0:T(8,128)(2,1)}) %all-reduce.2.cloned.1.call-update) | async-done | bytes 4194320 | tf_op jit(solution)/shard_map/psum | solution.py:104
  288.7 6.0 %multiply_reduce_fusion = (f32[1024]{0:T(1024)S(1)}, f32[1024]{0:T(1024)S(1)}) fusion(bf16[1024,2048]{1,0:T(8,128)(2,1)} %all-reduce.2.cloned.1.call-done, bf16[1024,2048]{1,0:T(8,128)(2,1)} %param.13, bf16[1024,2048]{1,0:T(8,128)(2,1)} %param.17), kind=kLoop, calls=%fused_computation.77 | loop fusion | flops 16775168 | bytes 12591104 | tf_op jit(solution)/shard_map/reduce_sum | solution.py:13
  307.1 97.3 %while.37 = (s32[]{:T(128)}, bf16[4,1024,512]{2,1,0:T(8,128)(2,1)}, s32[4]{0:T(128)S(1)}, s32[4096]{0:T(1024)S(1)}, s32[1024]{0:T(1024)S(1)}, /*index=5*/bf16[40...) while((s32[]{:T(128)}, bf16[4,1024,512]{2,1,0:T(8,128)(2,1)}, ...), condition=%wide.region_12.13_spmd.clone, body=%wide.region_11.12_spmd.clone.sunk | while | flops 2178418688 | bytes 40952544 | solution.py:166
  315.4 8.0 %fusion.153 = bf16[2,1024,128]{1,2,0:T(8,128)(2,1)S(1)} fusion(bf16[2,1024,128]{1,2,0:T(8,128)(2,1)S(1)} %get-tuple-element.903, f32[2,1024,1024]{2,1,0:T(8,128)} %fusion.151, f32[2,1024]{1,0:T(2,128)S(1)} %get-tuple-element.907, f32[2,1024]{1,0:T(2,128)S(1)} %get-tuple-element.904, pred[1024,1024]{0,1:T(8,128)(4,1)S(1)} %compare_and_fusion.6, ...), kind=kOutput, calls=%fused_computation.17.clone.1 | convolution fusion | flops 1088946176 | bytes 11550720 | tf_op jit(solution)/shard_map/while/body/eval_jaxpr/hqk,hqe->khe/dot_general | solution.py:138
  323.4 6.3 %fusion.152 = bf16[2,1024,128]{1,2,0:T(8,128)(2,1)S(1)} fusion(bf16[2,1024,128]{1,2,0:T(8,128)(2,1)} %get-tuple-element.906, f32[2,1024,1024]{2,1,0:T(8,128)} %fusion.151, f32[2,1024]{1,0:T(2,128)S(1)} %get-tuple-element.904, pred[1024,1024]{0,1:T(8,128)(4,1)S(1)} %compare_and_fusion.6), kind=kOutput, calls=%fused_computation.10.clone.1 | convolution fusion | flops 547356672 | bytes 10493952 | tf_op jit(solution)/shard_map/while/body/eval_jaxpr/hqk,hqe->khe/dot_general | solution.py:134
  339.7 8.0 %fusion.153 = bf16[2,1024,128]{1,2,0:T(8,128)(2,1)S(1)} fusion(bf16[2,1024,128]{1,2,0:T(8,128)(2,1)S(1)} %get-tuple-element.903, f32[2,1024,1024]{2,1,0:T(8,128)} %fusion.151, f32[2,1024]{1,0:T(2,128)S(1)} %get-tuple-element.907, f32[2,1024]{1,0:T(2,128)S(1)} %get-tuple-element.904, pred[1024,1024]{0,1:T(8,128)(4,1)S(1)} %compare_and_fusion.6, ...), kind=kOutput, calls=%fused_computation.17.clone.1 | convolution fusion | flops 1088946176 | bytes 11550720 | tf_op jit(solution)/shard_map/while/body/eval_jaxpr/hqk,hqe->khe/dot_general | solution.py:138
  347.7 6.3 %fusion.152 = bf16[2,1024,128]{1,2,0:T(8,128)(2,1)S(1)} fusion(bf16[2,1024,128]{1,2,0:T(8,128)(2,1)} %get-tuple-element.906, f32[2,1024,1024]{2,1,0:T(8,128)} %fusion.151, f32[2,1024]{1,0:T(2,128)S(1)} %get-tuple-element.904, pred[1024,1024]{0,1:T(8,128)(4,1)S(1)} %compare_and_fusion.6), kind=kOutput, calls=%fused_computation.10.clone.1 | convolution fusion | flops 547356672 | bytes 10493952 | tf_op jit(solution)/shard_map/while/body/eval_jaxpr/hqk,hqe->khe/dot_general | solution.py:134
  364.1 8.0 %fusion.153 = bf16[2,1024,128]{1,2,0:T(8,128)(2,1)S(1)} fusion(bf16[2,1024,128]{1,2,0:T(8,128)(2,1)S(1)} %get-tuple-element.903, f32[2,1024,1024]{2,1,0:T(8,128)} %fusion.151, f32[2,1024]{1,0:T(2,128)S(1)} %get-tuple-element.907, f32[2,1024]{1,0:T(2,128)S(1)} %get-tuple-element.904, pred[1024,1024]{0,1:T(8,128)(4,1)S(1)} %compare_and_fusion.6, ...), kind=kOutput, calls=%fused_computation.17.clone.1 | convolution fusion | flops 1088946176 | bytes 11550720 | tf_op jit(solution)/shard_map/while/body/eval_jaxpr/hqk,hqe->khe/dot_general | solution.py:138
  372.1 6.3 %fusion.152 = bf16[2,1024,128]{1,2,0:T(8,128)(2,1)S(1)} fusion(bf16[2,1024,128]{1,2,0:T(8,128)(2,1)} %get-tuple-element.906, f32[2,1024,1024]{2,1,0:T(8,128)} %fusion.151, f32[2,1024]{1,0:T(2,128)S(1)} %get-tuple-element.904, pred[1024,1024]{0,1:T(8,128)(4,1)S(1)} %compare_and_fusion.6), kind=kOutput, calls=%fused_computation.10.clone.1 | convolution fusion | flops 547356672 | bytes 10493952 | tf_op jit(solution)/shard_map/while/body/eval_jaxpr/hqk,hqe->khe/dot_general | solution.py:134
  388.3 8.0 %fusion.153 = bf16[2,1024,128]{1,2,0:T(8,128)(2,1)S(1)} fusion(bf16[2,1024,128]{1,2,0:T(8,128)(2,1)S(1)} %get-tuple-element.903, f32[2,1024,1024]{2,1,0:T(8,128)} %fusion.151, f32[2,1024]{1,0:T(2,128)S(1)} %get-tuple-element.907, f32[2,1024]{1,0:T(2,128)S(1)} %get-tuple-element.904, pred[1024,1024]{0,1:T(8,128)(4,1)S(1)} %compare_and_fusion.6, ...), kind=kOutput, calls=%fused_computation.17.clone.1 | convolution fusion | flops 1088946176 | bytes 11550720 | tf_op jit(solution)/shard_map/while/body/eval_jaxpr/hqk,hqe->khe/dot_general | solution.py:138
  396.4 6.3 %fusion.152 = bf16[2,1024,128]{1,2,0:T(8,128)(2,1)S(1)} fusion(bf16[2,1024,128]{1,2,0:T(8,128)(2,1)} %get-tuple-element.906, f32[2,1024,1024]{2,1,0:T(8,128)} %fusion.151, f32[2,1024]{1,0:T(2,128)S(1)} %get-tuple-element.904, pred[1024,1024]{0,1:T(8,128)(4,1)S(1)} %compare_and_fusion.6), kind=kOutput, calls=%fused_computation.10.clone.1 | convolution fusion | flops 547356672 | bytes 10493952 | tf_op jit(solution)/shard_map/while/body/eval_jaxpr/hqk,hqe->khe/dot_general | solution.py:134
  404.5 71.0 %while.39 = (s32[]{:T(128)}, f32[2,1024,128]{2,1,0:T(8,128)}, s32[4]{0:T(128)S(1)}, s32[4,1024]{1,0:T(4,128)S(1)}, s32[1024]{0:T(1024)S(1)}, /*index=5*/bf16[4,1...) while((s32[]{:T(128)}, f32[2,1024,128]{2,1,0:T(8,128)}, ...), condition=%wide.region_10.11_spmd.clone, body=%wide.region_9.10_spmd.clone.sunk | while | flops 1629227008 | bytes 27836616 | solution.py:33
  408.5 4.8 fusion.169
  413.2 9.0 %fusion.170 = f32[2,1024,128]{2,1,0:T(8,128)} fusion(bf16[1024,2,128]{0,2,1:T(8,128)(2,1)S(1)} %bitcast.223, f32[2,1024,1024]{2,1,0:T(8,128)} %fusion.169, f32[2,1024]{1,0:T(2,128)S(1)} %get-tuple-element.861, f32[2,1024]{1,0:T(2,128)S(1)} %get-tuple-element.858, pred[1024,1024]{0,1:T(8,128)(4,1)S(1)} %compare_and_fusion.8, ...), kind=kOutput, calls=%fused_computation.63.clone.1 | convolution fusion | flops 1089208320 | bytes 13123585 | tf_op jit(solution)/shard_map/while/body/eval_jaxpr/hqk,khe->hqe/dot_general | solution.py:142
  430.6 9.4 %fusion.170 = f32[2,1024,128]{2,1,0:T(8,128)} fusion(bf16[1024,2,128]{0,2,1:T(8,128)(2,1)S(1)} %bitcast.223, f32[2,1024,1024]{2,1,0:T(8,128)} %fusion.169, f32[2,1024]{1,0:T(2,128)S(1)} %get-tuple-element.861, f32[2,1024]{1,0:T(2,128)S(1)} %get-tuple-element.858, pred[1024,1024]{0,1:T(8,128)(4,1)S(1)} %compare_and_fusion.8, ...), kind=kOutput, calls=%fused_computation.63.clone.1 | convolution fusion | flops 1089208320 | bytes 13123585 | tf_op jit(solution)/shard_map/while/body/eval_jaxpr/hqk,khe->hqe/dot_general | solution.py:142
  448.3 9.4 %fusion.170 = f32[2,1024,128]{2,1,0:T(8,128)} fusion(bf16[1024,2,128]{0,2,1:T(8,128)(2,1)S(1)} %bitcast.223, f32[2,1024,1024]{2,1,0:T(8,128)} %fusion.169, f32[2,1024]{1,0:T(2,128)S(1)} %get-tuple-element.861, f32[2,1024]{1,0:T(2,128)S(1)} %get-tuple-element.858, pred[1024,1024]{0,1:T(8,128)(4,1)S(1)} %compare_and_fusion.8, ...), kind=kOutput, calls=%fused_computation.63.clone.1 | convolution fusion | flops 1089208320 | bytes 13123585 | tf_op jit(solution)/shard_map/while/body/eval_jaxpr/hqk,khe->hqe/dot_general | solution.py:142
  466.0 9.3 %fusion.170 = f32[2,1024,128]{2,1,0:T(8,128)} fusion(bf16[1024,2,128]{0,2,1:T(8,128)(2,1)S(1)} %bitcast.223, f32[2,1024,1024]{2,1,0:T(8,128)} %fusion.169, f32[2,1024]{1,0:T(2,128)S(1)} %get-tuple-element.861, f32[2,1024]{1,0:T(2,128)S(1)} %get-tuple-element.858, pred[1024,1024]{0,1:T(8,128)(4,1)S(1)} %compare_and_fusion.8, ...), kind=kOutput, calls=%fused_computation.63.clone.1 | convolution fusion | flops 1089208320 | bytes 13123585 | tf_op jit(solution)/shard_map/while/body/eval_jaxpr/hqk,khe->hqe/dot_general | solution.py:142
  476.9 5.8 %fusion.85 = f32[1024,2048]{1,0:T(8,128)} fusion(bf16[1024,256]{0,1:T(8,128)(2,1)S(1)} %bitcast.238, bf16[3,2048,256]{2,1,0:T(8,128)(2,1)} %param.15), kind=kOutput, calls=%fused_computation.96 | convolution fusion | flops 1073741824 | bytes 9961472 | tf_op jit(solution)/shard_map/sn,dn->sd/dot_general | solution.py:182
  491.5 6.6 %convert_element_type.75 = f32[1024,2048]{1,0:T(8,128)} convert(bf16[1024,2048]{1,0:T(8,128)(2,1)} %param.13) | non-fusion elementwise | flops 2097152 | bytes 12582912 | tf_op jit(solution)/shard_map/convert_element_type | solution.py:45
  498.9 42.9 %reduce-scatter.5.cloned.1.call-done = bf16[128,2048]{1,0:T(8,128)(2,1)} async-done(((bf16[1024,2048]{1,0:T(8,128)(2,1)}), bf16[128,2048]{1,0:T(8,128)(2,1)}) %reduce-scatter.5.cloned.1.call-update) | async-done | bytes 524304 | tf_op jit(solution)/shard_map/reduce_scatter | solution.py:186
  (189 shorter events, 170.6 us)
Async XLA Ops:
  6.5 182.3 %copy-start = (bf16[256,2048]{1,0:T(8,128)(2,1)S(1)}, bf16[256,2048]{1,0:T(8,128)(2,1)}, u32[]{:S(2)}) copy-start(bf16[256,2048]{1,0:T(8,128)(2,1)} %param.16) | copy-start | bytes 3145732
  6.5 50.1 %all-gather.5.cloned.1.call-start = ((), (), s32[]{:S(2)}) async-start(), calls=%async_computation.5 | async-start | bytes 2621440 | tf_op jit(solution)/shard_map/all_gather | solution.py:91
  7.3 10.0 %copy-start.13 = (f32[2048]{0:T(1024)}, f32[2048]{0:T(1024)S(1)}, u32[]{:S(2)}) copy-start(f32[2048]{0:T(1024)S(1)} %convert_element_type.76) | copy-start | bytes 24580
  10.4 7.0 %copy-start.15 = (f32[1024]{0:T(1024)}, f32[1024]{0:T(1024)S(1)}, u32[]{:S(2)}) copy-start(f32[1024]{0:T(1024)S(1)} %add_rsqrt_fusion.1) | copy-start | bytes 12292
  10.4 9.2 %copy-start.10 = (s32[1024]{0:T(1024)S(1)}, s32[1024]{0:T(1024)}, u32[]{:S(2)}) copy-start(s32[1024]{0:T(1024)} %param.19) | copy-start | bytes 12292
  18.5 75.1 %all-gather.7.cloned.1.call-start = ((), (), s32[]{:S(2)}) async-start(), calls=%async_computation.6 | async-start | bytes 2621440 | tf_op jit(solution)/shard_map/all_gather | solution.py:92
  19.3 269.4 %all-reduce.2.cloned.1.call-start = ((), (), s32[]{:S(2)}) async-start(), calls=%async_computation.2 | async-start | bytes 8388608 | tf_op jit(solution)/shard_map/psum | solution.py:104
  111.5 5.8 %copy-start.2 = (f32[2,1024,1024]{2,1,0:T(8,128)S(1)}, f32[2,1024,1024]{2,1,0:T(8,128)}, u32[]{:S(2)}) copy-start(f32[2,1024,1024]{2,1,0:T(8,128)} %get-tuple-element.764) | copy-start | bytes 25165828 | tf_op jit(solution)/shard_map/while
  111.5 5.9 %copy-start.8 = (bf16[1,1024,256]{1,2,0:T(8,128)(2,1)S(1)}, bf16[1,1024,256]{1,2,0:T(8,128)(2,1)}, u32[]{:S(2)}) copy-start(bf16[1,1024,256]{1,2,0:T(8,128)(2,1)} %get-tuple-element.766) | copy-start | bytes 1572868 | tf_op jit(solution)/shard_map/while
  131.5 5.8 %copy-start.2 = (f32[2,1024,1024]{2,1,0:T(8,128)S(1)}, f32[2,1024,1024]{2,1,0:T(8,128)}, u32[]{:S(2)}) copy-start(f32[2,1024,1024]{2,1,0:T(8,128)} %get-tuple-element.764) | copy-start | bytes 25165828 | tf_op jit(solution)/shard_map/while
  131.5 5.9 %copy-start.8 = (bf16[1,1024,256]{1,2,0:T(8,128)(2,1)S(1)}, bf16[1,1024,256]{1,2,0:T(8,128)(2,1)}, u32[]{:S(2)}) copy-start(bf16[1,1024,256]{1,2,0:T(8,128)(2,1)} %get-tuple-element.766) | copy-start | bytes 1572868 | tf_op jit(solution)/shard_map/while
  152.6 5.8 %copy-start.2 = (f32[2,1024,1024]{2,1,0:T(8,128)S(1)}, f32[2,1024,1024]{2,1,0:T(8,128)}, u32[]{:S(2)}) copy-start(f32[2,1024,1024]{2,1,0:T(8,128)} %get-tuple-element.764) | copy-start | bytes 25165828 | tf_op jit(solution)/shard_map/while
  152.6 5.9 %copy-start.8 = (bf16[1,1024,256]{1,2,0:T(8,128)(2,1)S(1)}, bf16[1,1024,256]{1,2,0:T(8,128)(2,1)}, u32[]{:S(2)}) copy-start(bf16[1,1024,256]{1,2,0:T(8,128)(2,1)} %get-tuple-element.766) | copy-start | bytes 1572868 | tf_op jit(solution)/shard_map/while
  173.6 5.8 %copy-start.2 = (f32[2,1024,1024]{2,1,0:T(8,128)S(1)}, f32[2,1024,1024]{2,1,0:T(8,128)}, u32[]{:S(2)}) copy-start(f32[2,1024,1024]{2,1,0:T(8,128)} %get-tuple-element.764) | copy-start | bytes 25165828 | tf_op jit(solution)/shard_map/while
  173.6 5.9 %copy-start.8 = (bf16[1,1024,256]{1,2,0:T(8,128)(2,1)S(1)}, bf16[1,1024,256]{1,2,0:T(8,128)(2,1)}, u32[]{:S(2)}) copy-start(bf16[1,1024,256]{1,2,0:T(8,128)(2,1)} %get-tuple-element.766) | copy-start | bytes 1572868 | tf_op jit(solution)/shard_map/while
  192.1 290.6 %reduce-scatter.3.cloned.1.call-start = ((), (), s32[]{:S(2)}) async-start(), calls=%async_computation.3 | async-start | bytes 5242880 | tf_op jit(solution)/shard_map/reduce_scatter | solution.py:167
  288.7 6.0 %copy-start.3 = (bf16[1024,2048]{1,0:T(8,128)(2,1)S(1)}, bf16[1024,2048]{1,0:T(8,128)(2,1)}, u32[]{:S(2)}) copy-start(bf16[1024,2048]{1,0:T(8,128)(2,1)} %param.13) | copy-start | bytes 12582916
  288.7 7.1 %copy-start.6 = (bf16[1024,2048]{1,0:T(8,128)(2,1)S(1)}, bf16[1024,2048]{1,0:T(8,128)(2,1)}, u32[]{:S(2)}) copy-start(bf16[1024,2048]{1,0:T(8,128)(2,1)} %param.17) | copy-start | bytes 12582916
  288.7 8.3 %copy-start.7 = (bf16[1024,2048]{1,0:T(8,128)(2,1)S(1)}, bf16[1024,2048]{1,0:T(8,128)(2,1)}, u32[]{:S(2)}) copy-start(bf16[1024,2048]{1,0:T(8,128)(2,1)} %all-reduce.2.cloned.1.call-done) | copy-start | bytes 12582916
  299.6 3.2 copy-start.5
  404.4 137.4 %reduce-scatter.5.cloned.1.call-start = ((), (), s32[]{:S(2)}) async-start(), calls=%async_computation.4 | async-start | bytes 4718592 | tf_op jit(solution)/shard_map/reduce_scatter | solution.py:186
  404.7 8.6 %copy-start.11 = (bf16[2,1024,128]{2,1,0:T(8,128)(2,1)S(1)}, bf16[2,1024,128]{2,1,0:T(8,128)(2,1)}, u32[]{:S(2)}) copy-start(bf16[2,1024,128]{2,1,0:T(8,128)(2,1)} %get-tuple-element.860) | copy-start | bytes 1572868 | tf_op jit(solution)/shard_map/while
  422.3 8.3 %copy-start.11 = (bf16[2,1024,128]{2,1,0:T(8,128)(2,1)S(1)}, bf16[2,1024,128]{2,1,0:T(8,128)(2,1)}, u32[]{:S(2)}) copy-start(bf16[2,1024,128]{2,1,0:T(8,128)(2,1)} %get-tuple-element.860) | copy-start | bytes 1572868 | tf_op jit(solution)/shard_map/while
  440.0 8.4 %copy-start.11 = (bf16[2,1024,128]{2,1,0:T(8,128)(2,1)S(1)}, bf16[2,1024,128]{2,1,0:T(8,128)(2,1)}, u32[]{:S(2)}) copy-start(bf16[2,1024,128]{2,1,0:T(8,128)(2,1)} %get-tuple-element.860) | copy-start | bytes 1572868 | tf_op jit(solution)/shard_map/while
  457.7 8.3 %copy-start.11 = (bf16[2,1024,128]{2,1,0:T(8,128)(2,1)S(1)}, bf16[2,1024,128]{2,1,0:T(8,128)(2,1)}, u32[]{:S(2)}) copy-start(bf16[2,1024,128]{2,1,0:T(8,128)(2,1)} %get-tuple-element.860) | copy-start | bytes 1572868 | tf_op jit(solution)/shard_map/while
  482.7 3.9 copy-start.4
  482.7 4.1 copy-start.9
  491.5 50.4 %copy-start.14 = (f32[2048]{0:T(1024)S(1)}, f32[2048]{0:T(1024)}, u32[]{:S(2)}) copy-start(f32[2048]{0:T(1024)} %copy-done.13) | copy-start | bytes 24580
  491.5 52.0 %copy-start.12 = (bf16[128,2048]{1,0:T(8,128)(2,1)S(1)}, bf16[128,2048]{1,0:T(8,128)(2,1)}, u32[]{:S(2)}) copy-start(bf16[128,2048]{1,0:T(8,128)(2,1)} %param.18) | copy-start | bytes 1572868
  491.5 55.1 %copy-start.1 = (bf16[256,2048]{1,0:T(8,128)(2,1)S(1)}, bf16[256,2048]{1,0:T(8,128)(2,1)}, u32[]{:S(2)}) copy-start(bf16[256,2048]{1,0:T(8,128)(2,1)} %param.16) | copy-start | bytes 3145732
Sparse Core Ops, SparseCore 0:
  18.6 37.8 all-gather.4
  58.4 35.1 all-gather.6
  192.2 96.4 all-reduce.1
  404.6 52.6 reduce-scatter.2
  491.6 50.1 reduce-scatter.4
where the time goes:
time: 559 us; the launch traced here: 553 us
  matrix products  198 us (35%)
  waiting for transfers between devices  196 us (35%)
  local copies, waits for them, and re-layouts  67.8 us (12%)
  other arithmetic  64.9 us (12%)
  between operations  13.6 us (2%)
  blocking collectives  9.97 us (2%)
    psum x1, waiting for transfers between devices, body(): lax.psum(term.astype(jnp.bfloat16), 'head').astype(jnp.float32)  96 us
    reduce_scatter x1, waiting for transfers between devices, body(): lax.psum_scatter((running + jnp.einsum('sn,dn->sd', value_grad, w_qkv[2],...  42.9 us
    dot_general x4, matrix products, back_block(): jnp.einsum('hqk,khe->hqe', dscore_half, key_heads, preferred_element_type...  37.1 us
    dot_general x8, matrix products, back_block(): jnp.einsum('hqe,khe->hqk', queries, key_heads, preferred_element_type=jnp...  36.6 us
    dot_general x4, matrix products, back_block(): jnp.einsum('hqk,hqe->khe', dscore_half, queries, preferred_element_type=j...  32 us
    all_gather x1, waiting for transfers between devices, body(): lax.all_gather(value_rows, 'ctx', axis=0, tiled=True)  28.9 us
    all_gather x1, waiting for transfers between devices, body(): lax.all_gather(key_rows, 'ctx', axis=0, tiled=True)  26.9 us
    dot_general x4, matrix products, back_block(): jnp.einsum('hqk,hqe->khe', prob_half, grads_out, preferred_element_type=j...  25.3 us
  transfers between devices with their start and end apart: 5, of which 4 were waited for; matrix products, arithmetic and copies ran while one was open for 17% of the time, Pallas kernels for 0%

commit v1 on v0

--- a/solution.py
+++ b/solution.py
@@ -7,6 +7,27 @@
 EPSILON = 1e-05
 STEP_SIZE = 0.25
 NEGATIVE = -1e30
+
+
+def in_order(blocks, dim):
+    blocks = jnp.moveaxis(blocks, 0, dim)
+    lengths = blocks.shape
+    return blocks.reshape(*lengths[:dim], lengths[dim] * lengths[dim + 1], *lengths[dim + 2 :])
+
+
+def grow_blocks(x, axis):
+    peers, mine = (lax.axis_size(axis), lax.axis_index(axis))
+    blocks, bit = (x[None], 1)
+    while bit < peers:
+        theirs = lax.ppermute(blocks, axis, [(i, i ^ bit) for i in range(peers)])
+        low = mine & bit == 0
+        blocks = jnp.concatenate([jnp.where(low, blocks, theirs), jnp.where(low, theirs, blocks)])
+        bit *= 2
+    return blocks
+
+
+def gather_by_bits(shard, axis, dim):
+    return in_order(grow_blocks(shard, axis), dim)
 
 
 def row_scale(matrix):
@@ -89,7 +110,7 @@
     )
     all_keys, all_values, all_segs = (
         lax.all_gather(key_rows, "ctx", axis=0, tiled=True),
-        lax.all_gather(value_rows, "ctx", axis=0, tiled=True),
+        gather_by_bits(value_rows, "ctx", 0),
         lax.all_gather(segment_ids, "ctx", axis=0, tiled=True),
     )
     run_max, run_sum, run_acc = over_blocks(

time: 559 us -> 542 us (0.970)
  waiting for transfers between devices: 196 us -> 152 us
  blocking collectives: 9.97 us -> 33.3 us
  local copies, waits for them, and re-layouts: 67.8 us -> 61.7 us
    all_gather x1 -> x0, waiting for transfers between devices: 28.9 us -> none  [body(): lax.all_gather(value_rows, 'ctx', axis=0, tiled=True)]
    all_gather x1, waiting for transfers between devices: 26.9 us -> 1.22 us  [body(): lax.all_gather(key_rows, 'ctx', axis=0, tiled=True)]
    all_gather x1, blocking collectives: 9.97 us -> 33.3 us  [body(): lax.all_gather(segment_ids, 'ctx', axis=0, tiled=True)]
    ppermute x0 -> x2, waiting for transfers between devices: none -> 11.9 us  [grow_blocks(): theirs = lax.ppermute(blocks, axis, [(i, i ^ bit) for i in range(peers)])]
    reshape x3 -> x1, local copies, waits for them, and re-layouts: 9.06 us -> 0.01 us  [over_blocks(): member.reshape((number, block_size) + member.shape[1:])]
    dot_general x4, matrix products: 20.6 us -> 15 us  [forward_block(): jnp.einsum('hqk,khe->hqe', weights.astype(jnp.bfloat16), value_heads, pre...]
    unnamed x29 -> x39, local copies, waits for them, and re-layouts: 16.1 us -> 16.8 us
  transfers between devices with their start and end apart: 5 -> 6, of which waited for: 4 -> 4; matrix products, arithmetic and copies ran while one was open for 17% -> 17% of each run, Pallas kernels for 0% -> 0%
where the time goes in v1:
time: 542 us; the launch traced here: 538 us
  matrix products  200 us (37%)
  waiting for transfers between devices  152 us (28%)
  other arithmetic  68 us (13%)
  local copies, waits for them, and re-layouts  61.7 us (11%)
  blocking collectives  33.3 us (6%)
  between operations  13.6 us (3%)
  starting transfers between devices  5.46 us (1%)
    psum x1, waiting for transfers between devices, body(): lax.psum(term.astype(jnp.bfloat16), 'head').astype(jnp.float32)  96.1 us
    reduce_scatter x1, waiting for transfers between devices, body(): lax.psum_scatter((running + jnp.einsum('sn,dn->sd', value_grad, w_qkv[2],...  43 us
    dot_general x8, matrix products, back_block(): jnp.einsum('hqe,khe->hqk', queries, key_heads, preferred_element_type=jnp...  40.8 us
    dot_general x4, matrix products, back_block(): jnp.einsum('hqk,khe->hqe', dscore_half, key_heads, preferred_element_type...  37.1 us
    all_gather x1, blocking collectives, body(): lax.all_gather(segment_ids, 'ctx', axis=0, tiled=True)  33.3 us
    dot_general x4, matrix products, back_block(): jnp.einsum('hqk,hqe->khe', dscore_half, queries, preferred_element_type=j...  32 us
    dot_general x4, matrix products, back_block(): jnp.einsum('hqk,hqe->khe', prob_half, grads_out, preferred_element_type=j...  25.4 us
    dot_general x4, matrix products, forward_block(): jnp.einsum('hqe,khe->hqk', queries, key_heads, preferred_element_type=jnp...  24.5 us
  transfers between devices with their start and end apart: 6, of which 4 were waited for; matrix products, arithmetic and copies ran while one was open for 17% of the time, Pallas kernels for 0%

profile of v1, /device:TPU:0, one launch (start us, length us, event | category | flops | bytes accessed | tf_op | source)
XLA Modules:
  0.0 537.8 jit_solution(16273113732715565183)
XLA Ops:
  10.4 6.6 %fusion.73 = bf16[3,1024,256]{2,1,0:T(8,128)(2,1)S(1)} fusion(bf16[3,2048,256]{2,1,0:T(8,128)(2,1)} %param.15, bf16[1024,2048]{1,0:T(8,128)(2,1)} %param.13, f32[2048]{0:T(1024)S(1)} %convert_element_type.76, f32[1024]{0:T(1024)S(1)} %add_rsqrt_fusion.1), kind=kOutput, calls=%fused_computation.91 | convolution fusion | flops 3230400512 | bytes 8925184 | tf_op jit(solution)/shard_map/sd,cdn->csn/dot_general | solution.py:70
  21.3 11.9 %collective-permute-done = bf16[1,1024,256]{2,1,0:T(8,128)(2,1)S(1)} collective-permute-done((bf16[1,1024,256]{2,1,0:T(8,128)(2,1)S(1)}, bf16[1,1024,256]{2,1,0:T(8,128)(2,1)S(1)}, u32[]{:S(2)}, u32[]{:S(2)}) %collective-permute-start) | collective-permute-done | bytes 524320 | tf_op jit(solution)/shard_map/ppermute | solution.py:22
  38.5 33.3 %all_gather.6 = s32[4096]{0:T(1024)S(1)} all-gather(s32[1024]{0:T(1024)S(1)} %copy-done.15), channel_id=1, replica_groups=mesh['ctx'=4,'head'=8] {'ctx'}, dimensions={0}, use_global_device_ids=true | all-gather | bytes 20480 | tf_op jit(solution)/shard_map/all_gather | solution.py:114
  82.5 82.1 %while.38 = (s32[]{:T(128)}, f32[2,1024]{1,0:T(2,128)S(1)}, f32[2,1024]{1,0:T(2,128)S(1)}, f32[2,1024,128]{2,1,0:T(8,128)}, s32[4]{0:T(128)S(1)}, /*index=5*/s32...) while((s32[]{:T(128)}, f32[2,1024]{1,0:T(2,128)S(1)}, ...), condition=%wide.region_4.5_spmd.clone, body=%wide.region_1.4_spmd.clone.sunk | while | flops 1104949248 | bytes 77234424 | solution.py:54
  86.1 6.1 %fusion.157 = (f32[2,1024]{1,0:T(2,128)S(1)}, f32[2,1024,1024]{2,1,0:T(8,128)}) fusion(pred[1024,1024]{0,1:T(8,128)(4,1)S(1)} %compare_and_fusion.7, bf16[1024,2,128]{0,2,1:T(8,128)(2,1)S(1)} %bitcast.227, bf16[2,1024,128]{2,1,0:T(8,128)(2,1)} %get-tuple-element.810), kind=kOutput, calls=%fused_computation.31.clone.1 | convolution fusion | flops 543160320 | bytes 10493952 | tf_op jit(solution)/shard_map/while/body/eval_jaxpr/hqe,khe->hqk/dot_general | solution.py:90
  106.6 6.1 %fusion.157 = (f32[2,1024]{1,0:T(2,128)S(1)}, f32[2,1024,1024]{2,1,0:T(8,128)}) fusion(pred[1024,1024]{0,1:T(8,128)(4,1)S(1)} %compare_and_fusion.7, bf16[1024,2,128]{0,2,1:T(8,128)(2,1)S(1)} %bitcast.227, bf16[2,1024,128]{2,1,0:T(8,128)(2,1)} %get-tuple-element.810), kind=kOutput, calls=%fused_computation.31.clone.1 | convolution fusion | flops 543160320 | bytes 10493952 | tf_op jit(solution)/shard_map/while/body/eval_jaxpr/hqe,khe->hqk/dot_general | solution.py:90
  127.1 6.1 %fusion.157 = (f32[2,1024]{1,0:T(2,128)S(1)}, f32[2,1024,1024]{2,1,0:T(8,128)}) fusion(pred[1024,1024]{0,1:T(8,128)(4,1)S(1)} %compare_and_fusion.7, bf16[1024,2,128]{0,2,1:T(8,128)(2,1)S(1)} %bitcast.227, bf16[2,1024,128]{2,1,0:T(8,128)(2,1)} %get-tuple-element.810), kind=kOutput, calls=%fused_computation.31.clone.1 | convolution fusion | flops 543160320 | bytes 10493952 | tf_op jit(solution)/shard_map/while/body/eval_jaxpr/hqe,khe->hqk/dot_general | solution.py:90
  147.7 6.1 %fusion.157 = (f32[2,1024]{1,0:T(2,128)S(1)}, f32[2,1024,1024]{2,1,0:T(8,128)}) fusion(pred[1024,1024]{0,1:T(8,128)(4,1)S(1)} %compare_and_fusion.7, bf16[1024,2,128]{0,2,1:T(8,128)(2,1)S(1)} %bitcast.227, bf16[2,1024,128]{2,1,0:T(8,128)(2,1)} %get-tuple-element.810), kind=kOutput, calls=%fused_computation.31.clone.1 | convolution fusion | flops 543160320 | bytes 10493952 | tf_op jit(solution)/shard_map/while/body/eval_jaxpr/hqe,khe->hqk/dot_general | solution.py:90
  171.4 96.1 %all-reduce.2.cloned.1.call-done = bf16[1024,2048]{1,0:T(8,128)(2,1)} async-done(((bf16[1024,2048]{1,0:T(8,128)(2,1)}), bf16[1024,2048]{1,0:T(8,128)(2,1)}) %all-reduce.2.cloned.1.call-update) | async-done | bytes 4194320 | tf_op jit(solution)/shard_map/psum | solution.py:125
  267.5 6.0 %multiply_reduce_fusion = (f32[1024]{0:T(1024)S(1)}, f32[1024]{0:T(1024)S(1)}) fusion(bf16[1024,2048]{1,0:T(8,128)(2,1)} %all-reduce.2.cloned.1.call-done, bf16[1024,2048]{1,0:T(8,128)(2,1)} %param.13, bf16[1024,2048]{1,0:T(8,128)(2,1)} %param.17), kind=kLoop, calls=%fused_computation.77 | loop fusion | flops 16775168 | bytes 12591104 | tf_op jit(solution)/shard_map/reduce_sum | solution.py:34
  285.9 103.1 %while.37 = (s32[]{:T(128)}, bf16[4,1024,512]{2,1,0:T(8,128)(2,1)}, s32[4]{0:T(128)S(1)}, s32[4096]{0:T(1024)S(1)}, s32[1024]{0:T(1024)S(1)}, /*index=5*/bf16[40...) while((s32[]{:T(128)}, bf16[4,1024,512]{2,1,0:T(8,128)(2,1)}, ...), condition=%wide.region_12.13_spmd.clone, body=%wide.region_11.12_spmd.clone.sunk | while | flops 2178418688 | bytes 45146872 | solution.py:187
  289.8 5.6 %fusion.150 = f32[2,1024,1024]{2,1,0:T(8,128)} fusion(bf16[1024,2,128]{0,2,1:T(8,128)(2,1)S(1)} %bitcast.221, bf16[2,1024,128]{1,2,0:T(8,128)(2,1)} %get-tuple-element.895), kind=kOutput, calls=%fused_computation.124.clone.1 | convolution fusion | flops 536870912 | bytes 9437184 | tf_op jit(solution)/shard_map/while/body/eval_jaxpr/hqe,khe->hqk/dot_general | solution.py:143
  295.6 8.0 %fusion.152 = bf16[2,1024,128]{1,2,0:T(8,128)(2,1)S(1)} fusion(bf16[2,1024,128]{1,2,0:T(8,128)(2,1)S(1)} %copy-done.8, f32[2,1024,1024]{2,1,0:T(8,128)} %fusion.150, f32[2,1024]{1,0:T(2,128)S(1)} %get-tuple-element.899, f32[2,1024]{1,0:T(2,128)S(1)} %get-tuple-element.896, pred[1024,1024]{0,1:T(8,128)(4,1)S(1)} %compare_and_fusion.6, ...), kind=kOutput, calls=%fused_computation.17.clone.1 | convolution fusion | flops 1088946176 | bytes 11550720 | tf_op jit(solution)/shard_map/while/body/eval_jaxpr/hqk,hqe->khe/dot_general | solution.py:159
  303.6 6.3 %fusion.151 = bf16[2,1024,128]{1,2,0:T(8,128)(2,1)S(1)} fusion(bf16[2,1024,128]{1,2,0:T(8,128)(2,1)} %get-tuple-element.898, f32[2,1024,1024]{2,1,0:T(8,128)} %fusion.150, f32[2,1024]{1,0:T(2,128)S(1)} %get-tuple-element.896, pred[1024,1024]{0,1:T(8,128)(4,1)S(1)} %compare_and_fusion.6), kind=kOutput, calls=%fused_computation.10.clone.1 | convolution fusion | flops 547356672 | bytes 10493952 | tf_op jit(solution)/shard_map/while/body/eval_jaxpr/hqk,hqe->khe/dot_general | solution.py:155
  315.5 5.6 %fusion.150 = f32[2,1024,1024]{2,1,0:T(8,128)} fusion(bf16[1024,2,128]{0,2,1:T(8,128)(2,1)S(1)} %bitcast.221, bf16[2,1024,128]{1,2,0:T(8,128)(2,1)} %get-tuple-element.895), kind=kOutput, calls=%fused_computation.124.clone.1 | convolution fusion | flops 536870912 | bytes 9437184 | tf_op jit(solution)/shard_map/while/body/eval_jaxpr/hqe,khe->hqk/dot_general | solution.py:143
  321.4 8.0 %fusion.152 = bf16[2,1024,128]{1,2,0:T(8,128)(2,1)S(1)} fusion(bf16[2,1024,128]{1,2,0:T(8,128)(2,1)S(1)} %copy-done.8, f32[2,1024,1024]{2,1,0:T(8,128)} %fusion.150, f32[2,1024]{1,0:T(2,128)S(1)} %get-tuple-element.899, f32[2,1024]{1,0:T(2,128)S(1)} %get-tuple-element.896, pred[1024,1024]{0,1:T(8,128)(4,1)S(1)} %compare_and_fusion.6, ...), kind=kOutput, calls=%fused_computation.17.clone.1 | convolution fusion | flops 1088946176 | bytes 11550720 | tf_op jit(solution)/shard_map/while/body/eval_jaxpr/hqk,hqe->khe/dot_general | solution.py:159
  329.4 6.3 %fusion.151 = bf16[2,1024,128]{1,2,0:T(8,128)(2,1)S(1)} fusion(bf16[2,1024,128]{1,2,0:T(8,128)(2,1)} %get-tuple-element.898, f32[2,1024,1024]{2,1,0:T(8,128)} %fusion.150, f32[2,1024]{1,0:T(2,128)S(1)} %get-tuple-element.896, pred[1024,1024]{0,1:T(8,128)(4,1)S(1)} %compare_and_fusion.6), kind=kOutput, calls=%fused_computation.10.clone.1 | convolution fusion | flops 547356672 | bytes 10493952 | tf_op jit(solution)/shard_map/while/body/eval_jaxpr/hqk,hqe->khe/dot_general | solution.py:155
  341.3 5.6 %fusion.150 = f32[2,1024,1024]{2,1,0:T(8,128)} fusion(bf16[1024,2,128]{0,2,1:T(8,128)(2,1)S(1)} %bitcast.221, bf16[2,1024,128]{1,2,0:T(8,128)(2,1)} %get-tuple-element.895), kind=kOutput, calls=%fused_computation.124.clone.1 | convolution fusion | flops 536870912 | bytes 9437184 | tf_op jit(solution)/shard_map/while/body/eval_jaxpr/hqe,khe->hqk/dot_general | solution.py:143
  347.1 8.0 %fusion.152 = bf16[2,1024,128]{1,2,0:T(8,128)(2,1)S(1)} fusion(bf16[2,1024,128]{1,2,0:T(8,128)(2,1)S(1)} %copy-done.8, f32[2,1024,1024]{2,1,0:T(8,128)} %fusion.150, f32[2,1024]{1,0:T(2,128)S(1)} %get-tuple-element.899, f32[2,1024]{1,0:T(2,128)S(1)} %get-tuple-element.896, pred[1024,1024]{0,1:T(8,128)(4,1)S(1)} %compare_and_fusion.6, ...), kind=kOutput, calls=%fused_computation.17.clone.1 | convolution fusion | flops 1088946176 | bytes 11550720 | tf_op jit(solution)/shard_map/while/body/eval_jaxpr/hqk,hqe->khe/dot_general | solution.py:159
  355.1 6.3 %fusion.151 = bf16[2,1024,128]{1,2,0:T(8,128)(2,1)S(1)} fusion(bf16[2,1024,128]{1,2,0:T(8,128)(2,1)} %get-tuple-element.898, f32[2,1024,1024]{2,1,0:T(8,128)} %fusion.150, f32[2,1024]{1,0:T(2,128)S(1)} %get-tuple-element.896, pred[1024,1024]{0,1:T(8,128)(4,1)S(1)} %compare_and_fusion.6), kind=kOutput, calls=%fused_computation.10.clone.1 | convolution fusion | flops 547356672 | bytes 10493952 | tf_op jit(solution)/shard_map/while/body/eval_jaxpr/hqk,hqe->khe/dot_general | solution.py:155
  367.1 5.6 %fusion.150 = f32[2,1024,1024]{2,1,0:T(8,128)} fusion(bf16[1024,2,128]{0,2,1:T(8,128)(2,1)S(1)} %bitcast.221, bf16[2,1024,128]{1,2,0:T(8,128)(2,1)} %get-tuple-element.895), kind=kOutput, calls=%fused_computation.124.clone.1 | convolution fusion | flops 536870912 | bytes 9437184 | tf_op jit(solution)/shard_map/while/body/eval_jaxpr/hqe,khe->hqk/dot_general | solution.py:143
  372.9 8.0 %fusion.152 = bf16[2,1024,128]{1,2,0:T(8,128)(2,1)S(1)} fusion(bf16[2,1024,128]{1,2,0:T(8,128)(2,1)S(1)} %copy-done.8, f32[2,1024,1024]{2,1,0:T(8,128)} %fusion.150, f32[2,1024]{1,0:T(2,128)S(1)} %get-tuple-element.899, f32[2,1024]{1,0:T(2,128)S(1)} %get-tuple-element.896, pred[1024,1024]{0,1:T(8,128)(4,1)S(1)} %compare_and_fusion.6, ...), kind=kOutput, calls=%fused_computation.17.clone.1 | convolution fusion | flops 1088946176 | bytes 11550720 | tf_op jit(solution)/shard_map/while/body/eval_jaxpr/hqk,hqe->khe/dot_general | solution.py:159
  380.9 6.3 %fusion.151 = bf16[2,1024,128]{1,2,0:T(8,128)(2,1)S(1)} fusion(bf16[2,1024,128]{1,2,0:T(8,128)(2,1)} %get-tuple-element.898, f32[2,1024,1024]{2,1,0:T(8,128)} %fusion.150, f32[2,1024]{1,0:T(2,128)S(1)} %get-tuple-element.896, pred[1024,1024]{0,1:T(8,128)(4,1)S(1)} %compare_and_fusion.6), kind=kOutput, calls=%fused_computation.10.clone.1 | convolution fusion | flops 547356672 | bytes 10493952 | tf_op jit(solution)/shard_map/while/body/eval_jaxpr/hqk,hqe->khe/dot_general | solution.py:155
  389.0 70.9 %while.39 = (s32[]{:T(128)}, f32[2,1024,128]{2,1,0:T(8,128)}, s32[4]{0:T(128)S(1)}, s32[4,1024]{1,0:T(4,128)S(1)}, s32[1024]{0:T(1024)S(1)}, /*index=5*/bf16[4,1...) while((s32[]{:T(128)}, f32[2,1024,128]{2,1,0:T(8,128)}, ...), condition=%wide.region_10.11_spmd.clone, body=%wide.region_9.10_spmd.clone.sunk | while | flops 1629227008 | bytes 27836616 | solution.py:54
  393.0 4.8 fusion.168
  397.8 9.0 %fusion.169 = f32[2,1024,128]{2,1,0:T(8,128)} fusion(bf16[1024,2,128]{0,2,1:T(8,128)(2,1)S(1)} %bitcast.220, f32[2,1024,1024]{2,1,0:T(8,128)} %fusion.168, f32[2,1024]{1,0:T(2,128)S(1)} %get-tuple-element.853, f32[2,1024]{1,0:T(2,128)S(1)} %get-tuple-element.850, pred[1024,1024]{0,1:T(8,128)(4,1)S(1)} %compare_and_fusion.8, ...), kind=kOutput, calls=%fused_computation.63.clone.1 | convolution fusion | flops 1089208320 | bytes 13123585 | tf_op jit(solution)/shard_map/while/body/eval_jaxpr/hqk,khe->hqe/dot_general | solution.py:163
  415.1 9.4 %fusion.169 = f32[2,1024,128]{2,1,0:T(8,128)} fusion(bf16[1024,2,128]{0,2,1:T(8,128)(2,1)S(1)} %bitcast.220, f32[2,1024,1024]{2,1,0:T(8,128)} %fusion.168, f32[2,1024]{1,0:T(2,128)S(1)} %get-tuple-element.853, f32[2,1024]{1,0:T(2,128)S(1)} %get-tuple-element.850, pred[1024,1024]{0,1:T(8,128)(4,1)S(1)} %compare_and_fusion.8, ...), kind=kOutput, calls=%fused_computation.63.clone.1 | convolution fusion | flops 1089208320 | bytes 13123585 | tf_op jit(solution)/shard_map/while/body/eval_jaxpr/hqk,khe->hqe/dot_general | solution.py:163
  432.8 9.4 %fusion.169 = f32[2,1024,128]{2,1,0:T(8,128)} fusion(bf16[1024,2,128]{0,2,1:T(8,128)(2,1)S(1)} %bitcast.220, f32[2,1024,1024]{2,1,0:T(8,128)} %fusion.168, f32[2,1024]{1,0:T(2,128)S(1)} %get-tuple-element.853, f32[2,1024]{1,0:T(2,128)S(1)} %get-tuple-element.850, pred[1024,1024]{0,1:T(8,128)(4,1)S(1)} %compare_and_fusion.8, ...), kind=kOutput, calls=%fused_computation.63.clone.1 | convolution fusion | flops 1089208320 | bytes 13123585 | tf_op jit(solution)/shard_map/while/body/eval_jaxpr/hqk,khe->hqe/dot_general | solution.py:163
  450.5 9.3 %fusion.169 = f32[2,1024,128]{2,1,0:T(8,128)} fusion(bf16[1024,2,128]{0,2,1:T(8,128)(2,1)S(1)} %bitcast.220, f32[2,1024,1024]{2,1,0:T(8,128)} %fusion.168, f32[2,1024]{1,0:T(2,128)S(1)} %get-tuple-element.853, f32[2,1024]{1,0:T(2,128)S(1)} %get-tuple-element.850, pred[1024,1024]{0,1:T(8,128)(4,1)S(1)} %compare_and_fusion.8, ...), kind=kOutput, calls=%fused_computation.63.clone.1 | convolution fusion | flops 1089208320 | bytes 13123585 | tf_op jit(solution)/shard_map/while/body/eval_jaxpr/hqk,khe->hqe/dot_general | solution.py:163
  461.4 5.8 %fusion.85 = f32[1024,2048]{1,0:T(8,128)} fusion(bf16[1024,256]{0,1:T(8,128)(2,1)S(1)} %bitcast.235, bf16[3,2048,256]{2,1,0:T(8,128)(2,1)} %param.15), kind=kOutput, calls=%fused_computation.98 | convolution fusion | flops 1073741824 | bytes 9961472 | tf_op jit(solution)/shard_map/sn,dn->sd/dot_general | solution.py:203
  475.9 6.6 %convert_element_type.75 = f32[1024,2048]{1,0:T(8,128)} convert(bf16[1024,2048]{1,0:T(8,128)(2,1)} %param.13) | non-fusion elementwise | flops 2097152 | bytes 12582912 | tf_op jit(solution)/shard_map/convert_element_type | solution.py:66
  483.3 43.0 %reduce-scatter.5.cloned.1.call-done = bf16[128,2048]{1,0:T(8,128)(2,1)} async-done(((bf16[1024,2048]{1,0:T(8,128)(2,1)}), bf16[128,2048]{1,0:T(8,128)(2,1)}) %reduce-scatter.5.cloned.1.call-update) | async-done | bytes 524304 | tf_op jit(solution)/shard_map/reduce_scatter | solution.py:207
  (228 shorter events, 165.4 us)
Async XLA Ops:
  6.5 159.8 %copy-start = (bf16[256,2048]{1,0:T(8,128)(2,1)S(1)}, bf16[256,2048]{1,0:T(8,128)(2,1)}, u32[]{:S(2)}) copy-start(bf16[256,2048]{1,0:T(8,128)(2,1)} %param.16) | copy-start | bytes 3145732
  6.5 71.9 %all-gather.3.cloned.1.call-start = ((), (), s32[]{:S(2)}) async-start(), calls=%async_computation.5 | async-start | bytes 2621440 | tf_op jit(solution)/shard_map/all_gather | solution.py:112
  7.3 9.8 %copy-start.20 = (f32[2048]{0:T(1024)}, f32[2048]{0:T(1024)S(1)}, u32[]{:S(2)}) copy-start(f32[2048]{0:T(1024)S(1)} %convert_element_type.76) | copy-start | bytes 24580
  10.4 6.7 %copy-start.22 = (f32[1024]{0:T(1024)}, f32[1024]{0:T(1024)S(1)}, u32[]{:S(2)}) copy-start(f32[1024]{0:T(1024)S(1)} %add_rsqrt_fusion.1) | copy-start | bytes 12292
  10.4 28.1 %copy-start.15 = (s32[1024]{0:T(1024)S(1)}, s32[1024]{0:T(1024)}, u32[]{:S(2)}) copy-start(s32[1024]{0:T(1024)} %param.19) | copy-start | bytes 12292
  18.3 15.0 %collective-permute-start = (bf16[1,1024,256]{2,1,0:T(8,128)(2,1)S(1)}, bf16[1,1024,256]{2,1,0:T(8,128)(2,1)S(1)}, u32[]{:S(2)}, u32[]{:S(2)}) collective-permute-start(bf16[1,1024,256]{2,1,0:T(8,128)(2,1)S(1)} %slice.36), channel_id=1, source_target_pairs={{0,8},{8,0},{16,24},{24,16},{1,9},{9,1},{17,25},{25,17},{2,10},{10... | collective-permute-start | bytes 1572872 | tf_op jit(solution)/shard_map/ppermute | solution.py:22
  35.6 231.9 %all-reduce.2.cloned.1.call-start = ((), (), s32[]{:S(2)}) async-start(), calls=%async_computation.2 | async-start | bytes 8388608 | tf_op jit(solution)/shard_map/psum | solution.py:125
  36.7 36.2 %collective-permute-start.1 = (bf16[2,1024,256]{2,1,0:T(8,128)(2,1)}, bf16[2,1024,256]{2,1,0:T(8,128)(2,1)}, u32[]{:S(2)}, u32[]{:S(2)}) collective-permute-start(bf16[2,1024,256]{2,1,0:T(8,128)(2,1)} %pad_maximum_fusion.1), channel_id=1, source_target_pairs={{0,16},{8,24},{16,0},{24,8},{1,17},{9,25},{17,1},{25,9},{2,18},{10... | collective-permute-start | bytes 3145736 | tf_op jit(solution)/shard_map/ppermute | solution.py:22
  74.5 8.0 %copy-start.6 = (bf16[4,1024,256]{2,1,0:T(8,128)(2,1)}, bf16[4,1024,256]{2,1,0:T(8,128)(2,1)S(1)}, u32[]{:S(2)}) copy-start(bf16[4,1024,256]{2,1,0:T(8,128)(2,1)S(1)} %pad_maximum_fusion) | copy-start | bytes 6291460
  92.2 5.8 %copy-start.2 = (f32[2,1024,1024]{2,1,0:T(8,128)S(1)}, f32[2,1024,1024]{2,1,0:T(8,128)}, u32[]{:S(2)}) copy-start(f32[2,1024,1024]{2,1,0:T(8,128)} %get-tuple-element.756) | copy-start | bytes 25165828 | tf_op jit(solution)/shard_map/while
  92.2 6.1 %copy-start.16 = (f32[2,1024,128]{2,1,0:T(8,128)S(1)}, f32[2,1024,128]{2,1,0:T(8,128)}, u32[]{:S(2)}) copy-start(f32[2,1024,128]{2,1,0:T(8,128)} %get-tuple-element.792) | copy-start | bytes 3145732 | tf_op jit(solution)/shard_map/while
  112.8 5.8 %copy-start.2 = (f32[2,1024,1024]{2,1,0:T(8,128)S(1)}, f32[2,1024,1024]{2,1,0:T(8,128)}, u32[]{:S(2)}) copy-start(f32[2,1024,1024]{2,1,0:T(8,128)} %get-tuple-element.756) | copy-start | bytes 25165828 | tf_op jit(solution)/shard_map/while
  112.8 6.1 %copy-start.16 = (f32[2,1024,128]{2,1,0:T(8,128)S(1)}, f32[2,1024,128]{2,1,0:T(8,128)}, u32[]{:S(2)}) copy-start(f32[2,1024,128]{2,1,0:T(8,128)} %get-tuple-element.792) | copy-start | bytes 3145732 | tf_op jit(solution)/shard_map/while
  133.3 6.1 %copy-start.16 = (f32[2,1024,128]{2,1,0:T(8,128)S(1)}, f32[2,1024,128]{2,1,0:T(8,128)}, u32[]{:S(2)}) copy-start(f32[2,1024,128]{2,1,0:T(8,128)} %get-tuple-element.792) | copy-start | bytes 3145732 | tf_op jit(solution)/shard_map/while
  153.8 6.1 %copy-start.16 = (f32[2,1024,128]{2,1,0:T(8,128)S(1)}, f32[2,1024,128]{2,1,0:T(8,128)}, u32[]{:S(2)}) copy-start(f32[2,1024,128]{2,1,0:T(8,128)} %get-tuple-element.792) | copy-start | bytes 3145732 | tf_op jit(solution)/shard_map/while
  169.7 297.5 %reduce-scatter.3.cloned.1.call-start = ((), (), s32[]{:S(2)}) async-start(), calls=%async_computation.3 | async-start | bytes 5242880 | tf_op jit(solution)/shard_map/reduce_scatter | solution.py:188
  267.5 6.0 %copy-start.3 = (bf16[1024,2048]{1,0:T(8,128)(2,1)S(1)}, bf16[1024,2048]{1,0:T(8,128)(2,1)}, u32[]{:S(2)}) copy-start(bf16[1024,2048]{1,0:T(8,128)(2,1)} %param.13) | copy-start | bytes 12582916
  267.5 7.1 %copy-start.9 = (bf16[1024,2048]{1,0:T(8,128)(2,1)S(1)}, bf16[1024,2048]{1,0:T(8,128)(2,1)}, u32[]{:S(2)}) copy-start(bf16[1024,2048]{1,0:T(8,128)(2,1)} %param.17) | copy-start | bytes 12582916
  267.5 8.3 %copy-start.10 = (bf16[1024,2048]{1,0:T(8,128)(2,1)S(1)}, bf16[1024,2048]{1,0:T(8,128)(2,1)}, u32[]{:S(2)}) copy-start(bf16[1024,2048]{1,0:T(8,128)(2,1)} %all-reduce.2.cloned.1.call-done) | copy-start | bytes 12582916
  285.9 103.1 %copy-start.7 = (bf16[2,1024,128]{2,1,0:T(8,128)(2,1)S(1)}, bf16[2,1024,128]{2,1,0:T(8,128)(2,1)}, u32[]{:S(2)}) copy-start(bf16[2,1024,128]{2,1,0:T(8,128)(2,1)} %get-tuple-element.913) | copy-start | bytes 1572868
  289.7 5.8 %copy-start.8 = (bf16[2,1024,128]{1,2,0:T(8,128)(2,1)S(1)}, bf16[2,1024,128]{1,2,0:T(8,128)(2,1)}, u32[]{:S(2)}) copy-start(bf16[2,1024,128]{1,2,0:T(8,128)(2,1)} %get-tuple-element.895) | copy-start | bytes 1572868 | tf_op jit(solution)/shard_map/while
  315.5 5.8 %copy-start.8 = (bf16[2,1024,128]{1,2,0:T(8,128)(2,1)S(1)}, bf16[2,1024,128]{1,2,0:T(8,128)(2,1)}, u32[]{:S(2)}) copy-start(bf16[2,1024,128]{1,2,0:T(8,128)(2,1)} %get-tuple-element.895) | copy-start | bytes 1572868 | tf_op jit(solution)/shard_map/while
  341.3 5.8 %copy-start.8 = (bf16[2,1024,128]{1,2,0:T(8,128)(2,1)S(1)}, bf16[2,1024,128]{1,2,0:T(8,128)(2,1)}, u32[]{:S(2)}) copy-start(bf16[2,1024,128]{1,2,0:T(8,128)(2,1)} %get-tuple-element.895) | copy-start | bytes 1572868 | tf_op jit(solution)/shard_map/while
  367.1 5.8 %copy-start.8 = (bf16[2,1024,128]{1,2,0:T(8,128)(2,1)S(1)}, bf16[2,1024,128]{1,2,0:T(8,128)(2,1)}, u32[]{:S(2)}) copy-start(bf16[2,1024,128]{1,2,0:T(8,128)(2,1)} %get-tuple-element.895) | copy-start | bytes 1572868 | tf_op jit(solution)/shard_map/while
  389.0 137.3 %reduce-scatter.5.cloned.1.call-start = ((), (), s32[]{:S(2)}) async-start(), calls=%async_computation.4 | async-start | bytes 4718592 | tf_op jit(solution)/shard_map/reduce_scatter | solution.py:207
  389.2 8.5 %copy-start.18 = (bf16[2,1024,128]{2,1,0:T(8,128)(2,1)S(1)}, bf16[2,1024,128]{2,1,0:T(8,128)(2,1)}, u32[]{:S(2)}) copy-start(bf16[2,1024,128]{2,1,0:T(8,128)(2,1)} %get-tuple-element.852) | copy-start | bytes 1572868 | tf_op jit(solution)/shard_map/while
  406.8 8.3 %copy-start.18 = (bf16[2,1024,128]{2,1,0:T(8,128)(2,1)S(1)}, bf16[2,1024,128]{2,1,0:T(8,128)(2,1)}, u32[]{:S(2)}) copy-start(bf16[2,1024,128]{2,1,0:T(8,128)(2,1)} %get-tuple-element.852) | copy-start | bytes 1572868 | tf_op jit(solution)/shard_map/while
  424.5 8.3 %copy-start.18 = (bf16[2,1024,128]{2,1,0:T(8,128)(2,1)S(1)}, bf16[2,1024,128]{2,1,0:T(8,128)(2,1)}, u32[]{:S(2)}) copy-start(bf16[2,1024,128]{2,1,0:T(8,128)(2,1)} %get-tuple-element.852) | copy-start | bytes 1572868 | tf_op jit(solution)/shard_map/while
  442.2 8.3 %copy-start.18 = (bf16[2,1024,128]{2,1,0:T(8,128)(2,1)S(1)}, bf16[2,1024,128]{2,1,0:T(8,128)(2,1)}, u32[]{:S(2)}) copy-start(bf16[2,1024,128]{2,1,0:T(8,128)(2,1)} %get-tuple-element.852) | copy-start | bytes 1572868 | tf_op jit(solution)/shard_map/while
  475.9 50.4 %copy-start.21 = (f32[2048]{0:T(1024)S(1)}, f32[2048]{0:T(1024)}, u32[]{:S(2)}) copy-start(f32[2048]{0:T(1024)} %copy-done.20) | copy-start | bytes 24580
  475.9 52.0 %copy-start.19 = (bf16[128,2048]{1,0:T(8,128)(2,1)S(1)}, bf16[128,2048]{1,0:T(8,128)(2,1)}, u32[]{:S(2)}) copy-start(bf16[128,2048]{1,0:T(8,128)(2,1)} %param.18) | copy-start | bytes 1572868
  475.9 55.1 %copy-start.1 = (bf16[256,2048]{1,0:T(8,128)(2,1)S(1)}, bf16[256,2048]{1,0:T(8,128)(2,1)}, u32[]{:S(2)}) copy-start(bf16[256,2048]{1,0:T(8,128)(2,1)} %param.16) | copy-start | bytes 3145732
  (12 other events, 35.9 us)
Sparse Core Ops, SparseCore 0:
  35.7 42.7 all-gather.2
  169.8 97.6 all-reduce.1
  389.1 52.6 reduce-scatter.2
  476.0 50.1 reduce-scatter.4
